TPU v7x, 64 devices: a 2x2x8 block of a 4x4x8 slice. The times are simulated.
64 devices in a mesh: dp: 4 (over x, y), ep: 16 (over z, core).
Axes of the slice: x: 2, y: 2, z: 8, core: 2. Of those that a mesh axis runs over, the one named last changes fastest.
The devices are a block of a 4x4x8 slice.
Arguments:
- tokens: bfloat16 [2, 64, 512, 1536], P(None, ('dp', 'ep')), parts along dimension 1
- expert_ids: int32 [2, 32768, 6], P(None, ('dp', 'ep')), parts along dimension 1
- route_weights: float32 [2, 32768, 6], P(None, ('dp', 'ep')), parts along dimension 1
- attn_norm: bfloat16 [1536], replicated
- w_query: bfloat16 [1536, 12, 128], replicated
- w_key: bfloat16 [1536, 12, 128], replicated
- w_value: bfloat16 [1536, 12, 128], replicated
- w_out: bfloat16 [12, 128, 1536], replicated
- ffn_norm: bfloat16 [1536], replicated
- w_gate: bfloat16 [64, 1536, 512], P('ep')
- w_up: bfloat16 [64, 1536, 512], P('ep')
- w_down: bfloat16 [64, 512, 1536], P('ep')
- shared_gate: bfloat16 [1536, 1024], replicated
- shared_up: bfloat16 [1536, 1024], replicated
- shared_down: bfloat16 [1024, 1536], replicated
Outputs:
- output: bfloat16 [2, 64, 512, 1536], P(None, ('dp', 'ep')), parts along dimension 1
There are 4 independent parts. A program takes and returns all parts, laid end to end along the dimension named above; an argument that names none is the same for every part.
All inputs are finite; a program needn't handle non-finite values.
Results may differ from a plain program's by a relative error of at most 0.00977376.
Values are sent between devices in bfloat16 or wider.
A program may use at most 768 MiB of HBM per device.

v0:
```python
import jax
import jax.numpy as jnp
from jax import lax
from jax.sharding import PartitionSpec as P

NORM_EPS = 1e-6
CAP_FACTOR = 2
SLOT_ALIGN = 8


def capacity_of(n_tok, top_count, experts):
    return SLOT_ALIGN * ((CAP_FACTOR * n_tok * top_count + SLOT_ALIGN * experts - 1) // (SLOT_ALIGN * experts))


def rms_norm(in_vals, norm_gain):
    wide_vals = in_vals.astype(jnp.float32)
    inv_rms = lax.rsqrt(jnp.mean(wide_vals * wide_vals, axis=-1, keepdims=True) + NORM_EPS)
    return (wide_vals * inv_rms * norm_gain.astype(jnp.float32)).astype(jnp.bfloat16)


def attention_block(seq_rows, attn_norm, w_query, w_key, w_value, w_out):
    normed = rms_norm(seq_rows, attn_norm)
    queries = jnp.einsum("...sd,dhe->...she", normed, w_query, preferred_element_type=jnp.float32).astype(jnp.bfloat16)
    key_rows = jnp.einsum("...sd,dhe->...she", normed, w_key, preferred_element_type=jnp.float32).astype(jnp.bfloat16)
    value_rows = jnp.einsum("...sd,dhe->...she", normed, w_value, preferred_element_type=jnp.float32).astype(jnp.bfloat16)
    seq_len = seq_rows.shape[-2]
    scores = jnp.einsum("...qhe,...khe->...hqk", queries, key_rows, preferred_element_type=jnp.float32) * (w_query.shape[-1] ** -0.5)
    causal = jnp.arange(seq_len)[:, None] >= jnp.arange(seq_len)[None, :]
    attn_probs = jax.nn.softmax(jnp.where(causal, scores, -jnp.inf), axis=-1).astype(jnp.bfloat16)
    head_mix = jnp.einsum("...hqk,...khe->...qhe", attn_probs, value_rows, preferred_element_type=jnp.float32).astype(jnp.bfloat16)
    attn_out = jnp.einsum("...qhe,hed->...qd", head_mix, w_out, preferred_element_type=jnp.float32)
    return (seq_rows.astype(jnp.float32) + attn_out).astype(jnp.bfloat16)


def swiglu(in_rows, gate_w, up_w, down_w):
    gate_act = jnp.dot(in_rows, gate_w, preferred_element_type=jnp.float32)
    up_act = jnp.dot(in_rows, up_w, preferred_element_type=jnp.float32)
    hidden = (jax.nn.silu(gate_act) * up_act).astype(jnp.bfloat16)
    return jnp.dot(hidden, down_w, preferred_element_type=jnp.float32).astype(jnp.bfloat16)


def route_plan(flat_ids, experts, slot_cap):
    n_rows = flat_ids.shape[0]
    sort_order = jnp.argsort(flat_ids, stable=True).astype(jnp.int32)
    counts = jnp.bincount(flat_ids, length=experts)
    starts = jnp.cumsum(counts) - counts
    sorted_rank = jnp.zeros((n_rows,), jnp.int32).at[sort_order].set(jnp.arange(n_rows, dtype=jnp.int32))
    slot_ids = sorted_rank - starts[flat_ids]
    src_pos = sort_order[jnp.minimum(starts[:, None] + jnp.arange(slot_cap)[None, :], n_rows - 1)]
    return slot_ids, src_pos


def solution(mesh):
    group_size = mesh.shape["ep"]

    def device_step(tokens, expert_ids, route_weights, attn_norm, w_query, w_key, w_value, w_out, ffn_norm, w_gate, w_up, w_down, shared_gate, shared_up, shared_down):
        n_micro, n_seq, seq_len, d_model = tokens.shape
        n_tok = n_seq * seq_len
        top_count = expert_ids.shape[-1]
        local_experts = w_gate.shape[0]
        experts = local_experts * group_size
        slot_cap = capacity_of(n_tok, top_count, experts)
        micro_outs = []
        for micro_idx in range(n_micro):
            residual = attention_block(tokens[micro_idx], attn_norm, w_query, w_key, w_value, w_out).reshape(n_tok, d_model)
            normed = rms_norm(residual, ffn_norm)
            shared_out = swiglu(normed, shared_gate, shared_up, shared_down)
            flat_ids = expert_ids[micro_idx].reshape(-1)
            slot_ids, src_pos = route_plan(flat_ids, experts, slot_cap)
            send_rows = jnp.take(normed, src_pos // top_count, axis=0)
            recv_rows = lax.all_to_all(send_rows, "ep", 0, 0, tiled=True)
            recv_rows = recv_rows.reshape(group_size, local_experts, slot_cap, d_model)
            gate_act = jnp.einsum("secd,edf->secf", recv_rows, w_gate, preferred_element_type=jnp.float32)
            up_act = jnp.einsum("secd,edf->secf", recv_rows, w_up, preferred_element_type=jnp.float32)
            hidden = (jax.nn.silu(gate_act) * up_act).astype(jnp.bfloat16)
            expert_out = jnp.einsum("secf,efd->secd", hidden, w_down, preferred_element_type=jnp.float32).astype(jnp.bfloat16)
            back_rows = lax.all_to_all(expert_out.reshape(experts, slot_cap, d_model), "ep", 0, 0, tiled=True)
            picked = jnp.take(back_rows.reshape(experts * slot_cap, d_model), flat_ids * slot_cap + slot_ids, axis=0)
            picked = picked.reshape(n_tok, top_count, d_model)
            routed = jnp.sum(picked.astype(jnp.float32) * route_weights[micro_idx][:, :, None], axis=1)
            layer_rows = residual.astype(jnp.float32) + shared_out.astype(jnp.float32) + routed
            micro_outs.append(layer_rows.astype(jnp.bfloat16).reshape(n_seq, seq_len, d_model))
        return jnp.stack(micro_outs)

    token_spec = P(None, ("dp", "ep"), None, None)
    route_spec = P(None, ("dp", "ep"), None)
    rep_spec = P()
    expert_spec = P("ep", None, None)
    in_specs = (token_spec, route_spec, route_spec, rep_spec, rep_spec, rep_spec, rep_spec, rep_spec, rep_spec, expert_spec, expert_spec, expert_spec, rep_spec, rep_spec, rep_spec)
    return jax.shard_map(device_step, mesh=mesh, in_specs=in_specs, out_specs=token_spec, check_vma=False)
```

profile of v0, /device:TPU:21, one launch (start us, length us, event | category | flops | bytes accessed | tf_op | source)
XLA Modules:
  0.0 2077.5 jit_solution(2493053972302887159)
XLA Ops:
  2.2 21.7 %scatter_custom_fusion = s32[64]{0:T(128)S(1)} fusion(s32[3072]{0:T(1024)S(1)} %bitcast.331, s32[3072]{0:T(1024)S(1)} %broadcast.564, s32[]{:T(128)} %constant.45.clone.1), kind=kCustom, calls=%fused_computation.296 | custom fusion | flops 3072 | bytes 260 | tf_op jit(solution)/shard_map/scatter-add | solution.py:45
  30.7 34.3 %gather_fusion = s32[6144]{0:T(1024)S(1)} fusion(s32[3072]{0:T(1024)S(1)} %get-tuple-element.9, s32[6144]{0:T(1024)S(1)} %broadcast_clamp_fusion.3), kind=kCustom, calls=%fused_computation.4 | custom fusion | bytes 73728 | tf_op jit(solution)/shard_map/gather | solution.py:49
  169.2 38.9 %gather_fusion.2 = bf16[6144,1536]{1,0:T(8,128)(2,1)} fusion(bf16[512,1536]{1,0:T(8,128)(2,1)} %get-tuple-element.143, s32[6144]{0:T(1024)S(1)} %broadcast_clamp_fusion.1), kind=kCustom, calls=%fused_computation.clone | custom fusion | bytes 37773312 | tf_op jit(solution)/shard_map/jit(_take)/gather | solution.py:70
  208.1 16.6 broadcast_select_fusion.1
  236.1 21.9 %scatter_custom_fusion.2 = s32[64]{0:T(128)S(1)} fusion(s32[3072]{0:T(1024)S(1)} %bitcast.332, s32[3072]{0:T(1024)} %copy-done.24, s32[]{:T(128)} %constant.45.clone.1), kind=kCustom, calls=%fused_computation.294 | custom fusion | flops 3072 | bytes 768 | tf_op jit(solution)/shard_map/scatter-add | solution.py:45
  264.8 34.3 %gather_fusion.1 = s32[6144]{0:T(1024)S(1)} fusion(s32[3072]{0:T(1024)S(1)} %get-tuple-element.10, s32[6144]{0:T(1024)S(1)} %broadcast_clamp_fusion.2), kind=kCustom, calls=%fused_computation.5 | custom fusion | bytes 73728 | tf_op jit(solution)/shard_map/gather | solution.py:49
  299.5 38.9 %gather_fusion.4 = bf16[6144,1536]{1,0:T(8,128)(2,1)} fusion(bf16[512,1536]{1,0:T(8,128)(2,1)} %get-tuple-element.144, s32[6144]{0:T(1024)S(1)} %broadcast_clamp_fusion), kind=kCustom, calls=%fused_computation.2.clone | custom fusion | bytes 37773312 | tf_op jit(solution)/shard_map/jit(_take)/gather | solution.py:70
  354.9 307.9 %all-to-all-done = bf16[64,96,1536]{2,1,0:T(8,128)(2,1)} async-done(((bf16[64,96,1536]{2,1,0:T(8,128)(2,1)}), bf16[64,96,1536]{2,1,0:T(8,128)(2,1)}, u32[]{:S(2)}, u32[]{:S(2)}) %all-to-all-start) | async-done | bytes 18874400 | tf_op jit(solution)/shard_map/all_to_all | solution.py:71
  670.0 18.2 fusion.6
  688.2 31.2 %convert_bitcast_fusion.1 = bf16[16,4,96,1536]{3,2,0,1:T(8,128)(2,1)} fusion(f32[4,16,96,512]{3,2,1,0:T(8,128)} %fusion.6, bf16[4,512,1536]{2,1,0:T(8,128)(2,1)} %param.30, bf16[16,4,96,1536]{3,2,1,0:T(8,128)(2,1)} %bitcast.74, bf16[4,1536,512]{2,1,0:T(8,128)(2,1)} %param.28), kind=kOutput, calls=%fused_computation.15 | convolution fusion | flops 19355664384 | bytes 62914560 | tf_op jit(solution)/shard_map/secf,efd->secd/dot_general | solution.py:76
  719.5 17.2 copy.30
  736.7 360.3 %all-to-all-done.2 = bf16[64,96,1536]{2,1,0:T(8,128)(2,1)} async-done(((bf16[64,96,1536]{2,1,0:T(8,128)(2,1)}), bf16[64,96,1536]{2,1,0:T(8,128)(2,1)}, u32[]{:S(2)}, u32[]{:S(2)}) %all-to-all-start.2) | async-done | bytes 18874400 | tf_op jit(solution)/shard_map/all_to_all | solution.py:71
  1104.3 18.3 fusion.2
  1122.6 31.2 %convert_bitcast_fusion = bf16[16,4,96,1536]{3,2,0,1:T(8,128)(2,1)} fusion(f32[4,16,96,512]{3,2,1,0:T(8,128)} %fusion.2, bf16[4,512,1536]{2,1,0:T(8,128)(2,1)} %param.30, bf16[16,4,96,1536]{3,2,1,0:T(8,128)(2,1)} %bitcast.162, bf16[4,1536,512]{2,1,0:T(8,128)(2,1)} %param.28), kind=kOutput, calls=%fused_computation.14 | convolution fusion | flops 19355664384 | bytes 62914560 | tf_op jit(solution)/shard_map/secf,efd->secd/dot_general | solution.py:76
  1153.8 17.2 copy.39
  1171.0 360.2 %all-to-all-done.1 = bf16[64,96,1536]{2,1,0:T(8,128)(2,1)} async-done(((bf16[64,96,1536]{2,1,0:T(8,128)(2,1)}), bf16[64,96,1536]{2,1,0:T(8,128)(2,1)}, u32[]{:S(2)}, u32[]{:S(2)}) %all-to-all-start.1) | async-done | bytes 18874400 | tf_op jit(solution)/shard_map/all_to_all | solution.py:77
  1581.9 35.7 %compare_and_fusion.3 = (pred[3072]{0:T(1024)(128)(4,1)S(1)}, s32[3072]{0:T(1024)S(1)}) fusion(s32[3072]{0:T(1024)S(1)} %scatter_custom_fusion.1, pred[3072]{0:T(1024)(128)(4,1)S(1)} %get-tuple-element.69, pred[3072]{0:T(1024)(128)(4,1)S(1)} %get-tuple-element.68, pred[3072]{0:T(1024)(128)(4,1)S(1)} %get-tuple-element.67, ...), kind=kLoop, calls=%fused_computation.279 | loop fusion | flops 202752 | bytes 227556 | tf_op jit(solution)/shard_map/jit(_take)/and | solution.py:78
  1617.6 35.4 %compare_and_fusion.2 = (pred[3072]{0:T(1024)(128)(4,1)S(1)}, s32[3072]{0:T(1024)S(1)}) fusion(s32[3072]{0:T(1024)S(1)} %scatter_custom_fusion.3, pred[3072]{0:T(1024)(128)(4,1)S(1)} %get-tuple-element.126, pred[3072]{0:T(1024)(128)(4,1)S(1)} %get-tuple-element.125, pred[3072]{0:T(1024)(128)(4,1)S(1)} %get-tuple-element.124, ...), kind=kLoop, calls=%fused_computation.278 | loop fusion | flops 202752 | bytes 227556 | tf_op jit(solution)/shard_map/jit(_take)/and | solution.py:78
  1661.7 28.3 %gather_fusion.3 = bf16[3072,1536]{1,0:T(8,128)(2,1)} fusion(bf16[6144,1536]{1,0:T(8,128)(2,1)} %bitcast.85, s32[3072]{0:T(1024)S(1)} %broadcast_clamp_fusion.5), kind=kCustom, calls=%fused_computation.1.clone | custom fusion | bytes 18886656 | tf_op jit(solution)/shard_map/jit(_take)/gather | solution.py:78
  1701.5 21.2 %reshape.500 = f32[512,6,1536]{2,1,0:T(8,128)} reshape(f32[3072,1536]{1,0:T(8,128)} %select_convert_fusion.1) | data formatting | bytes 37748736 | tf_op jit(solution)/shard_map/convert_element_type | solution.py:80
  1722.7 242.6 %all-to-all-done.3 = bf16[64,96,1536]{2,1,0:T(8,128)(2,1)} async-done(((bf16[64,96,1536]{2,1,0:T(8,128)(2,1)}), bf16[64,96,1536]{2,1,0:T(8,128)(2,1)}, u32[]{:S(2)}, u32[]{:S(2)}) %all-to-all-start.3) | async-done | bytes 18874400 | tf_op jit(solution)/shard_map/all_to_all | solution.py:77
  1965.3 28.1 %gather_fusion.5 = bf16[3072,1536]{1,0:T(8,128)(2,1)} fusion(bf16[6144,1536]{1,0:T(8,128)(2,1)} %bitcast.170, s32[3072]{0:T(1024)S(1)} %broadcast_clamp_fusion.4), kind=kCustom, calls=%fused_computation.3.clone | custom fusion | bytes 18886656 | tf_op jit(solution)/shard_map/jit(_take)/gather | solution.py:78
  2004.8 21.2 %reshape.502 = f32[512,6,1536]{2,1,0:T(8,128)} reshape(f32[3072,1536]{1,0:T(8,128)} %select_convert_fusion) | data formatting | bytes 37748736 | tf_op jit(solution)/shard_map/convert_element_type | solution.py:80
  2026.0 16.8 multiply_reduce_fusion.1
  (157 shorter events, 278.7 us)
Async XLA Ops:
  0.0 2055.3 %copy-start = (bf16[1024,1536]{1,0:T(8,128)(2,1)S(1)}, bf16[1024,1536]{1,0:T(8,128)(2,1)}, u32[]{:S(2)}) copy-start(bf16[1024,1536]{1,0:T(8,128)(2,1)} %param.33) | copy-start | bytes 9437188
  1.9 22.0 %copy-start.18 = (s32[3072,1]{0,1:T(1,128)}, s32[3072,1]{0,1:T(1,128)S(1)}, u32[]{:S(2)}) copy-start(s32[3072,1]{0,1:T(1,128)S(1)} %reshape_squeeze.11) | copy-start | bytes 36868
  2.0 63.0 %copy-start.16 = (s32[3072]{0:T(1024)}, s32[3072]{0:T(1024)S(1)}, u32[]{:S(2)}) copy-start(s32[3072]{0:T(1024)S(1)} %reshape_squeeze.10) | copy-start | bytes 36868
  2.2 21.7 %copy-start.24 = (s32[3072]{0:T(1024)}, s32[3072]{0:T(1024)S(1)}, u32[]{:S(2)}) copy-start(s32[3072]{0:T(1024)S(1)} %broadcast.564) | copy-start | bytes 36868
  30.7 34.3 %copy-start.1 = (s32[3072]{0:T(1024)}, s32[3072]{0:T(1024)S(1)}, u32[]{:S(2)}) copy-start(s32[3072]{0:T(1024)S(1)} %get-tuple-element.9) | copy-start | bytes 36868
  65.1 9.4 slice-start
  102.6 16.3 copy-start.8
  224.7 10.9 copy-start.22
  224.7 438.1 %all-to-all-start = ((bf16[64,96,1536]{2,1,0:T(8,128)(2,1)}), bf16[64,96,1536]{2,1,0:T(8,128)(2,1)}, u32[]{:S(2)}, u32[]{:S(2)}) async-start(bf16[64,96,1536]{2,1,0:T(8,128)(2,1)} %broadcast_select_fusion.1), calls=%async_computation | async-start | bytes 37748736 | tf_op jit(solution)/shard_map/all_to_all | solution.py:71
  235.9 63.2 %copy-start.20 = (s32[3072,1]{0,1:T(1,128)}, s32[3072,1]{0,1:T(1,128)S(1)}, u32[]{:S(2)}) copy-start(s32[3072,1]{0,1:T(1,128)S(1)} %reshape_squeeze.13) | copy-start | bytes 36868
  236.1 63.0 %copy-start.14 = (s32[3072]{0:T(1024)}, s32[3072]{0:T(1024)S(1)}, u32[]{:S(2)}) copy-start(s32[3072]{0:T(1024)S(1)} %reshape_squeeze.12) | copy-start | bytes 36868
  264.8 34.3 %copy-start.3 = (s32[3072]{0:T(1024)}, s32[3072]{0:T(1024)S(1)}, u32[]{:S(2)}) copy-start(s32[3072]{0:T(1024)S(1)} %get-tuple-element.10) | copy-start | bytes 36868
  662.8 434.2 %all-to-all-start.2 = ((bf16[64,96,1536]{2,1,0:T(8,128)(2,1)}), bf16[64,96,1536]{2,1,0:T(8,128)(2,1)}, u32[]{:S(2)}, u32[]{:S(2)}) async-start(bf16[64,96,1536]{2,1,0:T(8,128)(2,1)} %broadcast_select_fusion), calls=%async_computation.2 | async-start | bytes 37748736 | tf_op jit(solution)/shard_map/all_to_all | solution.py:71
  1097.0 434.3 %all-to-all-start.1 = ((bf16[64,96,1536]{2,1,0:T(8,128)(2,1)}), bf16[64,96,1536]{2,1,0:T(8,128)(2,1)}, u32[]{:S(2)}, u32[]{:S(2)}) async-start(bf16[64,96,1536]{2,1,0:T(8,128)(2,1)} %bitcast.324), calls=%async_computation.1 | async-start | bytes 37748736 | tf_op jit(solution)/shard_map/all_to_all | solution.py:77
  1531.3 19.6 copy-start.4
  1531.3 31.6 %copy-start.10 = (s32[64]{0:T(128)S(1)}, s32[64]{0:T(128)}, u32[]{:S(2)}) copy-start(s32[64]{0:T(128)} %copy-done.9) | copy-start | bytes 772
  1531.3 32.3 %copy-start.12 = (s32[64]{0:T(128)S(1)}, s32[64]{0:T(128)}, u32[]{:S(2)}) copy-start(s32[64]{0:T(128)} %copy-done.11) | copy-start | bytes 772
  1531.3 37.4 %copy-start.19 = (s32[3072,1]{0,1:T(1,128)S(1)}, s32[3072,1]{0,1:T(1,128)}, u32[]{:S(2)}) copy-start(s32[3072,1]{0,1:T(1,128)} %copy-done.18) | copy-start | bytes 36868
  1531.3 43.9 %copy-start.21 = (s32[3072,1]{0,1:T(1,128)S(1)}, s32[3072,1]{0,1:T(1,128)}, u32[]{:S(2)}) copy-start(s32[3072,1]{0,1:T(1,128)} %copy-done.20) | copy-start | bytes 36868
  1531.3 50.6 %copy-start.17 = (s32[3072]{0:T(1024)S(1)}, s32[3072]{0:T(1024)}, u32[]{:S(2)}) copy-start(s32[3072]{0:T(1024)} %copy-done.16) | copy-start | bytes 36868
  1531.3 86.2 %copy-start.15 = (s32[3072]{0:T(1024)S(1)}, s32[3072]{0:T(1024)}, u32[]{:S(2)}) copy-start(s32[3072]{0:T(1024)} %copy-done.14) | copy-start | bytes 36868
  1531.3 434.0 %all-to-all-start.3 = ((bf16[64,96,1536]{2,1,0:T(8,128)(2,1)}), bf16[64,96,1536]{2,1,0:T(8,128)(2,1)}, u32[]{:S(2)}, u32[]{:S(2)}) async-start(bf16[64,96,1536]{2,1,0:T(8,128)(2,1)} %bitcast.323), calls=%async_computation.3 | async-start | bytes 37748736 | tf_op jit(solution)/shard_map/all_to_all | solution.py:77
  2026.0 16.8 copy-start.6
  2026.0 16.8 copy-start.13
  (10 other events, 46.6 us)
where the time goes:
time: 2090 us; the launch traced here: 2080 us
  waiting for transfers between devices  1270 us (61%)
  local copies, waits for them, and re-layouts  317 us (15%)
  other arithmetic  259 us (12%)
  matrix products  198 us (9%)
  starting transfers between devices  32.1 us (2%)
    all_to_all x2, waiting for transfers between devices, device_step(): recv_rows = lax.all_to_all(send_rows, 'ep', 0, 0, tiled=True)  668 us
    all_to_all x2, waiting for transfers between devices, device_step(): lax.all_to_all(expert_out.reshape(experts, slot_cap, d_model), 'ep', 0, 0...  603 us
    gather x2, local copies, waits for them, and re-layouts, device_step(): send_rows = jnp.take(normed, src_pos // top_count, axis=0)  77.9 us
    and x2, other arithmetic, device_step(): jnp.take(back_rows.reshape(experts * slot_cap, d_model), flat_ids * slot_...  71 us
    gather x2, local copies, waits for them, and re-layouts, route_plan(): sort_order[jnp.minimum(starts[:, None] + jnp.arange(slot_cap)[None, :], n...  68.6 us
    dot_general x2, matrix products, device_step(): jnp.einsum('secf,efd->secd', hidden, w_down, preferred_element_type=jnp.f...  62.5 us
    gather x2, local copies, waits for them, and re-layouts, device_step(): jnp.take(back_rows.reshape(experts * slot_cap, d_model), flat_ids * slot_...  56.4 us
    scatter-add x2, other arithmetic, route_plan(): counts = jnp.bincount(flat_ids, length=experts)  43.6 us
  transfers between devices with their start and end apart: 4, of which 4 were waited for; matrix products, arithmetic and copies ran while one was open for 21% of the time, Pallas kernels for 0%

commit v1 on v0

v1 whole, which is shorter than its diff:
```python
import functools

import jax
import jax.numpy as jnp
from jax import lax
from jax.experimental import pallas as pl
from jax.experimental.pallas import tpu as pltpu
from jax.sharding import PartitionSpec as P

NORM_EPS = 1e-6
CHUNKS = 2


def rms_norm(in_vals, norm_gain):
    wide_vals = in_vals.astype(jnp.float32)
    inv_rms = lax.rsqrt(jnp.mean(wide_vals * wide_vals, axis=-1, keepdims=True) + NORM_EPS)
    return (wide_vals * inv_rms * norm_gain.astype(jnp.float32)).astype(jnp.bfloat16)


def attention_block(seq_rows, attn_norm, w_query, w_key, w_value, w_out):
    normed = rms_norm(seq_rows, attn_norm)
    queries = jnp.einsum("...sd,dhe->...she", normed, w_query, preferred_element_type=jnp.float32).astype(jnp.bfloat16)
    key_rows = jnp.einsum("...sd,dhe->...she", normed, w_key, preferred_element_type=jnp.float32).astype(jnp.bfloat16)
    value_rows = jnp.einsum("...sd,dhe->...she", normed, w_value, preferred_element_type=jnp.float32).astype(jnp.bfloat16)
    seq_len = seq_rows.shape[-2]
    scores = jnp.einsum("...qhe,...khe->...hqk", queries, key_rows, preferred_element_type=jnp.float32) * (w_query.shape[-1] ** -0.5)
    causal = jnp.arange(seq_len)[:, None] >= jnp.arange(seq_len)[None, :]
    attn_probs = jax.nn.softmax(jnp.where(causal, scores, -jnp.inf), axis=-1).astype(jnp.bfloat16)
    head_mix = jnp.einsum("...hqk,...khe->...qhe", attn_probs, value_rows, preferred_element_type=jnp.float32).astype(jnp.bfloat16)
    attn_out = jnp.einsum("...qhe,hed->...qd", head_mix, w_out, preferred_element_type=jnp.float32)
    return (seq_rows.astype(jnp.float32) + attn_out).astype(jnp.bfloat16)


def swiglu(in_rows, gate_w, up_w, down_w):
    gate_act = jnp.dot(in_rows, gate_w, preferred_element_type=jnp.float32)
    up_act = jnp.dot(in_rows, up_w, preferred_element_type=jnp.float32)
    hidden = (jax.nn.silu(gate_act) * up_act).astype(jnp.bfloat16)
    return jnp.dot(hidden, down_w, preferred_element_type=jnp.float32).astype(jnp.bfloat16)


def expert_body(z_ref, w_ref, gate_ref, up_ref, down_ref, out_ref):
    rows = z_ref.shape[0] * z_ref.shape[1]
    z_rows = z_ref[...].reshape(rows, z_ref.shape[2])
    w_rows = w_ref[...].reshape(rows, w_ref.shape[2])
    for e in range(gate_ref.shape[0]):
        gate_act = jnp.dot(z_rows, gate_ref[e], preferred_element_type=jnp.float32)
        up_act = jnp.dot(z_rows, up_ref[e], preferred_element_type=jnp.float32)
        hidden = (jax.nn.silu(gate_act) * up_act).astype(jnp.bfloat16)
        rows_out = jnp.dot(hidden, down_ref[e], preferred_element_type=jnp.float32).astype(jnp.bfloat16)
        w_col = w_rows[:, e : e + 1]
        term = jnp.where(w_col > 0, rows_out.astype(jnp.float32) * w_col, 0.0)
        term = term.reshape(out_ref.shape)
        if e == 0:
            out_ref[...] = term
        else:
            out_ref[...] += term


def expert_sums(z_all, w_all, w_gate, w_up, w_down, part, parts):
    n_src, n_tok, d_model = z_all.shape
    local = w_gate.shape[0]
    ff = w_gate.shape[2]
    rows = n_tok // parts
    srcs = parts
    flops = 6 * n_src * rows * d_model * ff * local
    return pl.pallas_call(
        expert_body,
        grid=(n_src // srcs,),
        out_shape=jax.ShapeDtypeStruct((n_src, rows, d_model), jnp.float32),
        in_specs=[
            pl.BlockSpec((srcs, rows, d_model), lambda i: (i, part, 0)),
            pl.BlockSpec((srcs, rows, local), lambda i: (i, part, 0)),
            pl.BlockSpec((local, d_model, ff), lambda i: (0, 0, 0), pipeline_mode=pl.Buffered(1)),
            pl.BlockSpec((local, d_model, ff), lambda i: (0, 0, 0), pipeline_mode=pl.Buffered(1)),
            pl.BlockSpec((local, ff, d_model), lambda i: (0, 0, 0), pipeline_mode=pl.Buffered(1)),
        ],
        out_specs=pl.BlockSpec((srcs, rows, d_model), lambda i: (i, 0, 0)),
        compiler_params=pltpu.CompilerParams(vmem_limit_bytes=52 * 1024 * 1024),
        cost_estimate=pl.CostEstimate(flops=flops, bytes_accessed=n_src * rows * d_model * 6, transcendentals=n_src * rows * ff * local),
        name="expert_sums",
    )(z_all, w_all, w_gate, w_up, w_down)


def solution(mesh):
    group_size = mesh.shape["ep"]

    def device_step(tokens, expert_ids, route_weights, attn_norm, w_query, w_key, w_value, w_out, ffn_norm, w_gate, w_up, w_down, shared_gate, shared_up, shared_down):
        n_micro, n_seq, seq_len, d_model = tokens.shape
        n_tok = n_seq * seq_len
        local_experts = w_gate.shape[0]
        experts = local_experts * group_size
        me = lax.axis_index("ep")
        hot = expert_ids[..., None] == jnp.arange(experts, dtype=jnp.int32)
        dense_w = jnp.sum(jnp.where(hot, route_weights[..., None], 0.0), axis=2)
        all_w = lax.all_gather(dense_w, "ep")
        my_w = lax.dynamic_slice_in_dim(all_w, me * local_experts, local_experts, axis=3)
        residuals, norms, gathered = [], [], []
        for m in range(n_micro):
            residual = attention_block(tokens[m], attn_norm, w_query, w_key, w_value, w_out).reshape(n_tok, d_model)
            normed = rms_norm(residual, ffn_norm)
            residuals.append(residual)
            norms.append(normed)
            gathered.append(lax.all_gather(normed, "ep"))
        micro_outs = []
        for m in range(n_micro):
            shared_out = swiglu(norms[m], shared_gate, shared_up, shared_down)
            pieces = []
            for c in range(CHUNKS):
                sums = expert_sums(gathered[m], my_w[:, m], w_gate, w_up, w_down, c, CHUNKS)
                pieces.append(lax.psum_scatter(sums, "ep", scatter_dimension=0))
            routed = jnp.concatenate(pieces, axis=0)
            layer_rows = residuals[m].astype(jnp.float32) + shared_out.astype(jnp.float32) + routed
            micro_outs.append(layer_rows.astype(jnp.bfloat16).reshape(n_seq, seq_len, d_model))
        return jnp.stack(micro_outs)

    token_spec = P(None, ("dp", "ep"), None, None)
    route_spec = P(None, ("dp", "ep"), None)
    rep_spec = P()
    expert_spec = P("ep", None, None)
    in_specs = (token_spec, route_spec, route_spec, rep_spec, rep_spec, rep_spec, rep_spec, rep_spec, rep_spec, expert_spec, expert_spec, expert_spec, rep_spec, rep_spec, rep_spec)
    return jax.shard_map(device_step, mesh=mesh, in_specs=in_specs, out_specs=token_spec, check_vma=False)
```

time: 2090 us -> 971 us (0.46)
  waiting for transfers between devices: 1270 us -> 445 us
  Pallas kernels: 0 us -> 358 us
  local copies, waits for them, and re-layouts: 317 us -> 10.2 us
  other arithmetic: 259 us -> 37.2 us
  matrix products: 198 us -> 99.9 us
  starting transfers between devices: 32.1 us -> 0.39 us
    all_to_all x4 -> x0, waiting for transfers between devices: 1270 us -> none  [the longest x2 668 us: device_step(): recv_rows = lax.all_to_all(send_rows, 'ep', 0, 0, tiled=True)]
    pallas_call x0 -> x4, Pallas kernels: none -> 358 us  [expert_sums(): pl.pallas_call(expert_body, grid=(n_src // srcs,), out_shape=jax.ShapeDty...]
    reduce_scatter x0 -> x4, waiting for transfers between devices: none -> 313 us  [device_step(): pieces.append(lax.psum_scatter(sums, 'ep', scatter_dimension=0))]
    gather x14 -> x0, local copies, waits for them, and re-layouts: 209 us -> none  [the longest x2 77.9 us: device_step(): send_rows = jnp.take(normed, src_pos // top_count, axis=0)]
    all_gather x0 -> x3, waiting for transfers between devices: none -> 131 us  [the longest x2 131 us: device_step(): gathered.append(lax.all_gather(normed, 'ep'))]
    dot_general x4 -> x0, matrix products: 98.9 us -> none  [the longest x2 62.5 us: device_step(): jnp.einsum('secf,efd->secd', hidden, w_down, preferred_element_type=jnp.f...]
    convert_element_type x4 -> x0, local copies, waits for them, and re-layouts: 76.9 us -> none  [the longest x2 42.5 us: device_step(): picked.astype(jnp.float32) * route_weights[micro_idx][:, :, None]]
    and x6 -> x0, other arithmetic: 71.1 us -> none  [the longest x2 71 us: device_step(): jnp.take(back_rows.reshape(experts * slot_cap, d_model), flat_ids * slot_...]
  transfers between devices with their start and end apart: 4 -> 7, of which waited for: 4 -> 4; matrix products, arithmetic and copies ran while one was open for 21% -> 14% of each run, Pallas kernels for 0% -> 37%
where the time goes in v1:
time: 971 us; the launch traced here: 965 us
  waiting for transfers between devices  445 us (46%)
  Pallas kernels  358 us (37%)
  matrix products  99.9 us (10%)
  other arithmetic  37.2 us (4%)
  between operations  14.2 us (1%)
  local copies, waits for them, and re-layouts  10.2 us (1%)
    pallas_call x4, Pallas kernels, expert_sums(): pl.pallas_call(expert_body, grid=(n_src // srcs,), out_shape=jax.ShapeDty...  358 us
    reduce_scatter x4, waiting for transfers between devices, device_step(): pieces.append(lax.psum_scatter(sums, 'ep', scatter_dimension=0))  313 us
    all_gather x2, waiting for transfers between devices, device_step(): gathered.append(lax.all_gather(normed, 'ep'))  131 us
    sub x2, other arithmetic, attention_block(): jax.nn.softmax(jnp.where(causal, scores, -jnp.inf), axis=-1)  27.2 us
    dot_general x2, matrix products, attention_block(): jnp.einsum('...qhe,...khe->...hqk', queries, key_rows, preferred_element_...  24.3 us
    dot_general x2, matrix products, attention_block(): jnp.einsum('...hqk,...khe->...qhe', attn_probs, value_rows, preferred_ele...  22.7 us
  transfers between devices with their start and end apart: 7, of which 4 were waited for; matrix products, arithmetic and copies ran while one was open for 14% of the time, Pallas kernels for 37%

profile of v1, /device:TPU:21, one launch (start us, length us, event | category | flops | bytes accessed | tf_op | source)
XLA Modules:
  0.0 964.9 jit_solution(1358867781697925851)
XLA Ops:
  12.2 6.2 convolution_convert_fusion.3
  18.4 12.2 %fusion.38 = f32[12,512,512]{1,2,0:T(8,128)} fusion(bf16[512,12,128]{2,0,1:T(8,128)(2,1)} %convolution_convert_fusion.3, bf16[1536,12,128]{2,0,1:T(8,128)(2,1)} %param.20, f32[512]{0:T(512)S(1)} %get-tuple-element.19, f32[1536]{0:T(1024)S(1)} %convert_element_type.179, bf16[2,1,512,1536]{3,2,1,0:T(8,128)(2,1)} %param.15), kind=kOutput, calls=%fused_computation.62 | convolution fusion | flops 3225157632 | bytes 20455424 | tf_op jit(solution)/shard_map/...qhe,...khe->...hqk/dot_general | solution.py:26
  30.6 13.6 %fusion.61 = (f32[12,512]{1,0:T(8,128)S(1)}, f32[12,512,512]{1,2,0:T(8,128)}) fusion(f32[12,512,512]{1,2,0:T(8,128)} %fusion.38, pred[512,512]{0,1:T(8,128)(4,1)S(1)} %iota_compare_fusion.1), kind=kOutput, calls=%fused_computation.89 | output fusion | flops 18874880 | bytes 25452544 | tf_op jit(solution)/shard_map/sub | solution.py:28
  44.2 11.3 %fusion.36 = bf16[12,128,512]{2,1,0:T(8,128)(2,1)} fusion(f32[12,512,512]{1,2,0:T(8,128)} %get-tuple-element.16, f32[12,512]{1,0:T(8,128)S(1)} %get-tuple-element.15, bf16[1536,12,128]{2,0,1:T(8,128)(2,1)} %param.21, f32[512]{0:T(512)S(1)} %get-tuple-element.19, f32[1536]{0:T(1024)S(1)} %convert_element_type.179, bf16[2,1,512,1536]{3,2,1,0:T(8,128)(2,1)} %param.15), kind=kOutput, calls=%fused_computation.59 | convolution fusion | flops 3232235520 | bytes 20480000 | tf_op jit(solution)/shard_map/...hqk,...khe->...qhe/dot_general | solution.py:29
  55.5 7.4 fusion.29
  63.0 6.2 convolution_convert_fusion.6
  69.2 12.2 %fusion.39 = f32[12,512,512]{1,2,0:T(8,128)} fusion(bf16[512,12,128]{2,0,1:T(8,128)(2,1)} %convolution_convert_fusion.6, bf16[1536,12,128]{2,0,1:T(8,128)(2,1)} %param.20, f32[1536]{0:T(1024)S(1)} %convert_element_type.179, f32[512]{0:T(512)S(1)} %get-tuple-element.20, bf16[2,1,512,1536]{3,2,1,0:T(8,128)(2,1)} %param.15), kind=kOutput, calls=%fused_computation.66 | convolution fusion | flops 3225157632 | bytes 20455424 | tf_op jit(solution)/shard_map/...qhe,...khe->...hqk/dot_general | solution.py:26
  81.3 13.6 %fusion.60 = (f32[12,512]{1,0:T(8,128)S(1)}, f32[12,512,512]{1,2,0:T(8,128)}) fusion(f32[12,512,512]{1,2,0:T(8,128)} %fusion.39, pred[512,512]{0,1:T(8,128)(4,1)S(1)} %iota_compare_fusion.1), kind=kOutput, calls=%fused_computation.88 | output fusion | flops 18874880 | bytes 25452544 | tf_op jit(solution)/shard_map/sub | solution.py:28
  94.9 11.3 %fusion.37 = bf16[12,128,512]{2,1,0:T(8,128)(2,1)} fusion(f32[12,512,512]{1,2,0:T(8,128)} %get-tuple-element.12, f32[12,512]{1,0:T(8,128)S(1)} %get-tuple-element.11, bf16[1536,12,128]{2,0,1:T(8,128)(2,1)} %param.21, f32[1536]{0:T(1024)S(1)} %convert_element_type.179, f32[512]{0:T(512)S(1)} %get-tuple-element.20, bf16[2,1,512,1536]{3,2,1,0:T(8,128)(2,1)} %param.15), kind=kOutput, calls=%fused_computation.60 | convolution fusion | flops 3232235520 | bytes 20480000 | tf_op jit(solution)/shard_map/...hqk,...khe->...qhe/dot_general | solution.py:29
  106.3 6.3 fusion.24
  117.8 3.1 copy.54
  120.9 130.9 %all-gather.7.cloned.1.call-done = bf16[8192,1536]{1,0:T(8,128)(2,1)} async-done(((bf16[512,1536]{1,0:T(8,128)(2,1)}), bf16[8192,1536]{1,0:T(8,128)(2,1)}) %all-gather.7.cloned.1.call-update) | async-done | bytes 25165840 | tf_op jit(solution)/shard_map/all_gather | solution.py:103
  251.8 89.3 %expert_sums.5 = f32[16,256,1536]{2,1,0:T(8,128)} custom-call(bf16[16,512,1536]{2,1,0:T(8,128)(2,1)} %bitcast.118, f32[16,512,4]{2,1,0:T(8,128)} %bitcast.111, bf16[4,1536,512]{2,1,0:T(8,128)(2,1)} %gate_ref.7, bf16[4,1536,512]{2,1,0:T(8,128)(2,1)} %up_ref.7, bf16[4,512,1536]{2,1,0:T(8,128)(2,1)} %down_ref.7), custom_call_target="tpu_custom_call" | custom-call | flops 77309411328 | bytes 37748736 | tf_op jit(solution)/shard_map/expert_sums/pallas_call | solution.py:66
  341.2 89.6 %expert_sums.4 = f32[16,256,1536]{2,1,0:T(8,128)} custom-call(bf16[16,512,1536]{2,1,0:T(8,128)(2,1)} %bitcast.119, f32[16,512,4]{2,1,0:T(8,128)} %bitcast.112, bf16[4,1536,512]{2,1,0:T(8,128)(2,1)} %gate_ref.7, bf16[4,1536,512]{2,1,0:T(8,128)(2,1)} %up_ref.7, bf16[4,512,1536]{2,1,0:T(8,128)(2,1)} %down_ref.7), custom_call_target="tpu_custom_call" | custom-call | flops 77309411328 | bytes 37748736 | tf_op jit(solution)/shard_map/expert_sums/pallas_call | solution.py:66
  434.5 89.3 %expert_sums.6 = f32[16,256,1536]{2,1,0:T(8,128)} custom-call(bf16[16,512,1536]{2,1,0:T(8,128)(2,1)} %bitcast.116, f32[16,512,4]{2,1,0:T(8,128)} %bitcast.113, bf16[4,1536,512]{2,1,0:T(8,128)(2,1)} %gate_ref.7, bf16[4,1536,512]{2,1,0:T(8,128)(2,1)} %up_ref.7, bf16[4,512,1536]{2,1,0:T(8,128)(2,1)} %down_ref.7), custom_call_target="tpu_custom_call" | custom-call | flops 77309411328 | bytes 37748736 | tf_op jit(solution)/shard_map/expert_sums/pallas_call | solution.py:66
  524.0 89.8 %expert_sums.7 = f32[16,256,1536]{2,1,0:T(8,128)} custom-call(bf16[16,512,1536]{2,1,0:T(8,128)(2,1)} %bitcast.117, f32[16,512,4]{2,1,0:T(8,128)} %bitcast.114, bf16[4,1536,512]{2,1,0:T(8,128)(2,1)} %gate_ref.7, bf16[4,1536,512]{2,1,0:T(8,128)(2,1)} %up_ref.7, bf16[4,512,1536]{2,1,0:T(8,128)(2,1)} %down_ref.7), custom_call_target="tpu_custom_call" | custom-call | flops 77309411328 | bytes 37748736 | tf_op jit(solution)/shard_map/expert_sums/pallas_call | solution.py:66
  613.9 5.7 fusion.62
  619.6 3.1 fusion.63
  622.7 40.9 %reduce-scatter.5.cloned.1.call-done = f32[1,256,1536]{2,1,0:T(8,128)} async-done(((f32[16,256,1536]{2,1,0:T(8,128)}), f32[1,256,1536]{2,1,0:T(8,128)}) %reduce-scatter.5.cloned.1.call-update) | async-done | bytes 1572880 | tf_op jit(solution)/shard_map/reduce_scatter | solution.py:110
  663.6 9.0 fusion.34
  672.5 131.6 %reduce-scatter.9.cloned.1.call-done = f32[1,256,1536]{2,1,0:T(8,128)} async-done(((f32[16,256,1536]{2,1,0:T(8,128)}), f32[1,256,1536]{2,1,0:T(8,128)}) %reduce-scatter.9.cloned.1.call-update) | async-done | bytes 1572880 | tf_op jit(solution)/shard_map/reduce_scatter | solution.py:110
  804.1 140.7 %reduce-scatter.11.cloned.1.call-done = f32[1,256,1536]{2,1,0:T(8,128)} async-done(((f32[16,256,1536]{2,1,0:T(8,128)}), f32[1,256,1536]{2,1,0:T(8,128)}) %reduce-scatter.11.cloned.1.call-update) | async-done | bytes 1572880 | tf_op jit(solution)/shard_map/reduce_scatter | solution.py:110
  944.8 9.0 fusion.35
  953.7 3.8 pad_maximum_fusion
  (50 shorter events, 14.7 us)
Async XLA Ops:
  6.5 657.0 %copy-start = (bf16[1024,1536]{1,0:T(8,128)(2,1)S(1)}, bf16[1024,1536]{1,0:T(8,128)(2,1)}, u32[]{:S(2)}) copy-start(bf16[1024,1536]{1,0:T(8,128)(2,1)} %param.29) | copy-start | bytes 9437188
  6.6 5.6 copy-start.7
  6.6 109.5 %all-gather.9.cloned.1.call-start = ((), (), s32[]{:S(2)}) async-start(), calls=%async_computation.9 | async-start | bytes 4456448 | tf_op jit(solution)/shard_map/all_gather | solution.py:95
  9.2 242.6 %all-gather.7.cloned.1.call-start = ((), (), s32[]{:S(2)}) async-start(), calls=%async_computation.8 | async-start | bytes 26738688 | tf_op jit(solution)/shard_map/all_gather | solution.py:103
  9.3 2.9 copy-start.1
  44.2 11.4 %copy-start.8 = (bf16[1536]{0:T(1024)(128)(2,1)S(1)}, bf16[1536]{0:T(1024)(128)(2,1)}, u32[]{:S(2)}) copy-start(bf16[1536]{0:T(1024)(128)(2,1)} %param.23) | copy-start | bytes 9220
  55.5 7.4 copy-start.2
  106.3 6.3 copy-start.4
  112.6 2.5 copy-start.5
  115.1 319.4 %all-gather.11.cloned.1.call-start = ((), (), s32[]{:S(2)}) async-start(), calls=%async_computation.10 | async-start | bytes 26738688 | tf_op jit(solution)/shard_map/all_gather | solution.py:103
  115.9 506.8 %reduce-scatter.7.cloned.1.call-start = ((), (), s32[]{:S(2)}) async-start(), calls=%async_computation.5 | async-start | bytes 26738688 | tf_op jit(solution)/shard_map/reduce_scatter | solution.py:110
  341.2 322.4 %reduce-scatter.5.cloned.1.call-start = ((), (), s32[]{:S(2)}) async-start(), calls=%async_computation.4 | async-start | bytes 26738688 | tf_op jit(solution)/shard_map/reduce_scatter | solution.py:110
  430.8 0.9 copy-start.6
  430.9 373.2 %reduce-scatter.9.cloned.1.call-start = ((), (), s32[]{:S(2)}) async-start(), calls=%async_computation.6 | async-start | bytes 26738688 | tf_op jit(solution)/shard_map/reduce_scatter | solution.py:110
  523.9 420.9 %reduce-scatter.11.cloned.1.call-start = ((), (), s32[]{:S(2)}) async-start(), calls=%async_computation.7 | async-start | bytes 26738688 | tf_op jit(solution)/shard_map/reduce_scatter | solution.py:110
  613.9 5.7 copy-start.3
  613.9 5.7 copy-start.9
Sparse Core Ops, SparseCore 0:
  9.4 43.6 all-gather.8
  115.2 136.5 all-gather.6
  253.4 130.0 all-gather.10
  385.7 137.2 reduce-scatter.6
  525.2 138.2 reduce-scatter.4
  665.8 138.2 reduce-scatter.8
  806.5 138.2 reduce-scatter.10
